TPU v7x, 32 devices: a whole 2x2x4 slice. The times are simulated.
32 devices in a mesh: section: 4 (over y, x), expert: 8 (over z, core).
Axes of the slice: x: 2, y: 2, z: 4, core: 2. Of those that a mesh axis runs over, the one named last changes fastest.
Arguments:
- tokens: bfloat16 [8, 64, 2048], P(None, 'expert'), may hold values from -6 to 6
- norm_gain: float32 [2, 2048], replicated, may hold values from 0.1 to 1.9
- w_gate: bfloat16 [4, 2048, 14336], P('section', None, 'expert'), may hold values from -0.125 to 0.125
- w_up: bfloat16 [4, 2048, 14336], P('section', None, 'expert'), may hold values from -0.125 to 0.125
- w_down: bfloat16 [4, 14336, 2048], P('section', 'expert'), may hold values from -0.0625 to 0.0625
- expert_ids: int32 [2, 8, 64, 2], P(None, None, 'expert'), may hold values from 0 to 3, as said below
- slot_ids: int32 [2, 8, 64, 2], P(None, None, 'expert'), may hold values from 0 to 4, as said below
- dropped: int32 [2, 8, 64, 2], P(None, None, 'expert'), may hold values from 0 to 1, as said below
- gate_weights: float32 [2, 8, 64, 2], P(None, None, 'expert'), may hold values from 0.1 to 1
Outputs:
- states: bfloat16 [4, 8, 64, 2048], P('section', None, 'expert')
Inputs may be any that keep to these rules, and one draw needn't show every extreme that they name: `expert_ids`: the two experts of a token differ. `slot_ids`: among the kept choices of the tokens of one index of expert that name one expert, the slots are 0, 1, ... up to their count less one, each once. At most 5 kept choices of the tokens of one index of expert name one expert, and a choice is dropped only where 5 kept choices of its index of expert name its expert; in each layer and micro-batch some expert receives exactly 5 kept choices from every index of expert.
All inputs are finite; a program needn't handle non-finite values.
Results may differ from a plain program's by a relative error of at most 0.025.
Values may be sent and summed in bfloat16 or wider, within the bound.
A program may use at most 64 MiB of HBM per device.

v0:
```python
import functools

import jax
import jax.numpy as jnp
from jax import lax
from jax.experimental import pallas as pl
from jax.experimental.pallas import tpu as pltpu
from jax.sharding import PartitionSpec as P

CORES = 2
TILE_ROWS = 16


def kernel(
    groups, layers, chunks, rows,
    tok, gain, pos_row, pos_col, weigh, gate_hbm, up_hbm, down_hbm,
    out,
    gate, up, down, rbuf, sbuf, pbuf, twin, rsum, retbuf, share_out, share_in, fbuf, xin, hid,
    wsem, disp_send, disp_recv, relay_send, twin_send, twin_recv, ret_send, ret_recv,
    share_send, share_recv, x_send, x_recv,
):
    chips = groups // CORES
    per_expert = chips // 2
    model_width = tok.shape[-1]
    width = gate.shape[-1]
    section = lax.axis_index("section")
    me = lax.axis_index("expert")
    layer = section // 2
    half = section % 2
    chip = me // CORES
    core = me % CORES
    sibling = me + 1 - 2 * core
    partner = section + 1 - 2 * half

    def fetch(i):
        src, dst = ((gate_hbm, gate), (up_hbm, up), (down_hbm, down))[i]
        return pltpu.make_async_copy(src.at[0], dst, wsem.at[i])

    def span(index, count=1):
        size = rows * count
        return pl.ds(pl.multiple_of(index * size, TILE_ROWS), size)

    def remote(src, dst, send, recv, **where):
        return pltpu.make_async_remote_copy(
            src_ref=src, dst_ref=dst, send_sem=send, recv_sem=recv,
            device_id=where, device_id_type=pl.DeviceIdType.MESH,
        )

    def chip_at(r):
        return lax.rem(chip + r, chips)

    def direct(c, r):
        there = chip_at(r)
        place = span(core * chips + chip)
        return remote(
            sbuf.at[c, span(there // per_expert)], rbuf.at[c, place], disp_send.at[c, r],
            disp_recv.at[c, core * chips + chip], expert=there * CORES + core,
        )

    def own_rows(c):
        place = core * chips + chip
        return remote(
            sbuf.at[c, span(chip // per_expert)], rbuf.at[c, span(place)], disp_send.at[c, 0],
            disp_recv.at[c, place], expert=sibling,
        )

    def relay(c, r):
        place = core * chips + chip_at(r)
        return remote(
            rbuf.at[c, span(place)], rbuf.at[c, span(place)], relay_send.at[c, r],
            disp_recv.at[c, place], expert=sibling,
        )

    def arrival(c, at_core, at_chip):
        place = at_core * chips + at_chip
        return remote(
            rbuf.at[c, span(place)], rbuf.at[c, span(place)], relay_send.at[c, 0],
            disp_recv.at[c, place], expert=sibling,
        )

    def to_twin(c):
        return remote(
            pbuf.at[c, span(1 - core, chips)], twin.at[c], twin_send.at[c], twin_recv.at[c], expert=sibling
        )

    def giving(c, r):
        there = chip_at(r)
        return remote(
            rsum.at[c, span(there)], retbuf.at[c, span(chip)], ret_send.at[c, r], ret_recv.at[c, chip],
            expert=there * CORES + core,
        )

    def given(c, r):
        there = chip_at(r)
        return remote(
            rsum.at[c, span(there)], retbuf.at[c, span(there)], ret_send.at[c, r], ret_recv.at[c, there],
            expert=there * CORES + core,
        )

    def swap(c):
        return remote(share_out.at[c], share_in.at[c], share_send.at[c], share_recv.at[c], section=partner)

    def hand_on(c):
        return remote(fbuf.at[c], xin.at[c], x_send.at[c], x_recv.at[c], section=lax.rem(section + 2, 2 * layers))

    def dispatch(c):
        current = xin[c].astype(jnp.float32)
        inv = lax.rsqrt(jnp.mean(current * current, axis=-1, keepdims=True) + 1e-05)
        normed = (current * inv * gain[...]).astype(jnp.bfloat16)
        slots = lax.broadcasted_iota(jnp.int32, (2 * rows, tok.shape[1]), 0)
        hot = (slots == pos_row[c, 0:1, :]) | (slots == pos_row[c, 1:2, :])
        place = jnp.where(hot, 1.0, 0.0).astype(jnp.bfloat16)
        sent = jnp.dot(place, normed, preferred_element_type=jnp.float32).astype(jnp.bfloat16)
        sbuf[c] = sent
        own = jnp.where(chip // per_expert == 0, sent[:rows], sent[rows:])
        rbuf[c, span(core * chips + chip), :] = own
        for r in range(chips - 1, 0, -1):
            direct(c, r).start()
        own_rows(c).start()

    def forward(c):
        for r in range(1, chips):
            arrival(c, core, chip_at(r)).wait_recv()
            relay(c, r).start()

    def compute(c):
        for r in range(chips):
            arrival(c, 1 - core, chip_at(r)).wait_recv()
        if c == 0:
            fetch(0).wait()
            fetch(1).wait()
        wide = 256 if width % 256 == 0 else 128

        def inner(t, carry):
            cols = pl.ds(pl.multiple_of(t * wide, wide), wide)
            got = rbuf[c]
            g = jnp.dot(got, gate[:, cols], preferred_element_type=jnp.float32)
            u = jnp.dot(got, up[:, cols], preferred_element_type=jnp.float32)
            hid[:, cols] = (g / (1.0 + jnp.exp(-g)) * u).astype(jnp.bfloat16)
            return carry

        lax.fori_loop(0, width // wide, inner, 0, unroll=True)
        if c == 0:
            fetch(2).wait()

        def outer(t, carry):
            cols = pl.ds(pl.multiple_of(t * 512, 512), 512)
            pbuf[c, :, cols] = jnp.dot(hid[...], down[:, cols], preferred_element_type=jnp.float32).astype(
                jnp.bfloat16
            )
            return carry

        lax.fori_loop(0, model_width // 512, outer, 0)
        to_twin(c).start()

    def pair(c):
        to_twin(c).wait_recv()
        mine = pbuf[c, span(core, chips), :].astype(jnp.float32)
        rsum[c] = (mine + twin[c].astype(jnp.float32)).astype(jnp.bfloat16)
        for r in range(chips - 1, 0, -1):
            giving(c, r).start()
        retbuf[c, span(chip), :] = rsum[c, span(chip), :]

    def combine(c):
        for r in range(1, chips):
            given(c, r).wait_recv()
        parts = []
        for j in range(2):
            total = jnp.zeros((rows, model_width), jnp.float32)
            for i in range(per_expert):
                low = (j * per_expert + i) * rows
                total = total + retbuf[c, low : low + rows, :].astype(jnp.float32)
            parts.append(total)
        made = jnp.concatenate(parts, axis=0)
        slots = lax.broadcasted_iota(jnp.int32, (tok.shape[1], 2 * rows), 1)
        spread = jnp.zeros((tok.shape[1], 2 * rows), jnp.float32)
        for k in range(2):
            spread = spread + jnp.where(slots == pos_col[c, :, k : k + 1], weigh[c, :, k : k + 1], 0.0)
        share = jnp.dot(spread, made, precision=lax.Precision.HIGHEST, preferred_element_type=jnp.float32)
        share_out[c] = share.astype(jnp.bfloat16)
        swap(c).start()
        out[c] = (xin[c].astype(jnp.float32) + share).astype(jnp.bfloat16)

    def finish(c):
        swap(c).wait_recv()
        both = share_out[c].astype(jnp.float32) + share_in[c].astype(jnp.float32)
        full = (xin[c].astype(jnp.float32) + both).astype(jnp.bfloat16)
        fbuf[c] = full

        @pl.when(layer < layers - 1)
        def _():
            hand_on(c).start()

        @pl.when(half == 1)
        def _():
            out[c] = full

    def first(c):
        if c < chunks:
            @pl.when(layer == 0)
            def _():
                xin[c] = tok[c]
                dispatch(c)

    def later(c):
        if c < chunks:
            @pl.when(layer > 0)
            def _():
                hand_on(c).wait_recv()
                dispatch(c)

    first(0)
    first(1)
    for i in range(3):
        fetch(i).start()
    later(0)
    forward(0)
    for c in range(chunks):
        compute(c)
        pair(c)
        first(c + 2)
        later(c + 1)
        if c >= 1:
            combine(c - 1)
        if c + 1 < chunks:
            forward(c + 1)
        if c >= 1:
            finish(c - 1)
    combine(chunks - 1)
    finish(chunks - 1)

    for c in range(chunks):
        own_rows(c).wait_send()
        to_twin(c).wait_send()
        swap(c).wait_send()
        for r in range(1, chips):
            direct(c, r).wait_send()
            relay(c, r).wait_send()
            giving(c, r).wait_send()

    @pl.when(layer < layers - 1)
    def _():
        for c in range(chunks):
            hand_on(c).wait_send()


def on_device(tokens, norm_gain, w_gate, w_up, w_down, expert_ids, slot_ids, dropped, gate_weights):
    groups = lax.axis_size("expert")
    layers = lax.axis_size("section") // 2
    section_at = lax.axis_index("section")
    local_count = 2
    micro_count, tok_rows, model_width = tokens.shape
    width = w_gate.shape[-1]
    capacity = 5 * tok_rows // (4 * local_count)
    layer_at, half_at = section_at // 2, section_at % 2
    per_chunk = max(1, TILE_ROWS // capacity)
    rows = -(-per_chunk * capacity // TILE_ROWS) * TILE_ROWS
    chunks = -(-micro_count // per_chunk)
    held = per_chunk * tok_rows
    lines = -(-held // TILE_ROWS) * TILE_ROWS
    chips = groups // CORES

    def chunked(value, fill):
        rest = value.shape[2:]
        extra = [(0, chunks * per_chunk - micro_count)] + [(0, 0)] * (value.ndim - 1)
        value = jnp.pad(value, extra, constant_values=fill).reshape((chunks, held) + rest)
        return jnp.pad(value, [(0, 0), (0, lines - held)] + [(0, 0)] * len(rest), constant_values=fill)

    def own_layer(value):
        return lax.dynamic_index_in_dim(value, layer_at, 0, keepdims=False)

    local_id = own_layer(expert_ids) - half_at * local_count
    owned = (own_layer(dropped) == 0) & (local_id >= 0) & (local_id < local_count)
    turn = (jnp.arange(micro_count, dtype=jnp.int32) % per_chunk)[:, None, None]
    position = jnp.where(owned, local_id * rows + turn * capacity + own_layer(slot_ids), -1)
    pos_col = chunked(position, -1)
    pos_row = jnp.transpose(pos_col, (0, 2, 1))
    weigh = chunked(own_layer(gate_weights), 0)
    gain_row = lax.dynamic_slice_in_dim(norm_gain, layer_at, 1, 0)

    vm = pl.BlockSpec(memory_space=pltpu.VMEM)
    hb = pl.BlockSpec(memory_space=pl.ANY)
    half16 = jnp.bfloat16
    dma = pltpu.SemaphoreType.DMA
    made = pl.pallas_call(
        functools.partial(kernel, groups, layers, chunks, rows),
        out_shape=jax.ShapeDtypeStruct((chunks, lines, model_width), half16),
        in_specs=[vm] * 5 + [hb] * 3,
        out_specs=vm,
        scratch_shapes=[
            pltpu.VMEM((model_width, width), half16),
            pltpu.VMEM((model_width, width), half16),
            pltpu.VMEM((width, model_width), half16),
            pltpu.VMEM((chunks, groups * rows, model_width), half16),
            pltpu.VMEM((chunks, 2 * rows, model_width), half16),
            pltpu.VMEM((chunks, groups * rows, model_width), half16),
            pltpu.VMEM((chunks, chips * rows, model_width), half16),
            pltpu.VMEM((chunks, chips * rows, model_width), half16),
            pltpu.VMEM((chunks, chips * rows, model_width), half16),
            pltpu.VMEM((chunks, lines, model_width), half16),
            pltpu.VMEM((chunks, lines, model_width), half16),
            pltpu.VMEM((chunks, lines, model_width), half16),
            pltpu.VMEM((chunks, lines, model_width), half16),
            pltpu.VMEM((groups * rows, width), half16),
            dma((3,)),
            dma((chunks, chips)),
            dma((chunks, groups)),
            dma((chunks, chips)),
            dma((chunks,)),
            dma((chunks,)),
            dma((chunks, chips)),
            dma((chunks, chips)),
            dma((chunks,)),
            dma((chunks,)),
            dma((chunks,)),
            dma((chunks,)),
        ],
        compiler_params=pltpu.CompilerParams(has_side_effects=True, vmem_limit_bytes=58 * 1024 * 1024),
    )(chunked(tokens, 0), gain_row, pos_row, pos_col, weigh, w_gate, w_up, w_down)
    made = made[:, :held].reshape(chunks * per_chunk, tok_rows, model_width)
    return made[None, :micro_count]


def solution(mesh):
    return jax.shard_map(
        on_device,
        mesh=mesh,
        in_specs=(
            P(None, "expert", None),
            P(),
            P("section", None, "expert"),
            P("section", None, "expert"),
            P("section", "expert", None),
            P(None, None, "expert", None),
            P(None, None, "expert", None),
            P(None, None, "expert", None),
            P(None, None, "expert", None),
        ),
        out_specs=P("section", None, "expert", None),
        check_vma=False,
    )
```

profile of v0, /device:TPU:6, one launch (start us, length us, event | category | flops | bytes accessed | tf_op | source)
XLA Modules:
  0.0 113.5 jit_solution(7487567516334428703)
XLA Ops:
  0.0 0.0 copy-start
  0.0 0.7 copy-done
  0.7 0.6 constant_dynamic-slice_fusion.4.gain
  1.3 0.7 constant_dynamic-slice_fusion.3
  2.0 0.7 constant_dynamic-slice_fusion
  2.7 0.7 constant_dynamic-slice_fusion.1
  3.4 0.1 fusion.1
  3.5 0.1 copy.21
  3.6 0.1 copy.23
  3.8 0.6 pad.29.weigh
  4.4 0.6 fusion.6
  5.0 0.7 copy.16.pos_row
  5.7 1.0 pad.24
  6.7 0.8 pad.25.tok
  7.5 104.3 %shard_map.91 = bf16[3,32,2048]{2,1,0:T(8,128)(2,1)} custom-call(bf16[3,32,2048]{2,1,0:T(8,128)(2,1)} %pad.25.tok, f32[1,2048]{1,0:T(1,128)} %constant_dynamic-slice_fusion.4.gain, s32[3,2,32]{2,1,0:T(2,128)} %copy.16.pos_row, s32[3,32,2]{2,1,0:T(8,128)} %get-tuple-element.5.pos_col, f32[3,32,2]{2,1,0:T(8,128)} %pad.29.weigh, ...), custom_call_target="tpu_custom_call" | custom-call | tf_op jit(solution)/shard_map/pallas_call | solution.py:285
  111.8 1.0 slice.6
  112.8 0.7 slice_bitcast_fusion
  (3 shorter events, 0.0 us)
Async XLA Ops:
  0.0 0.7 copy-start
where the time goes:
time: 115 us; the launch traced here: 114 us
  Pallas kernels  104 us (90%)
  local copies, waits for them, and re-layouts  9.07 us (8%)
    pallas_call x1, Pallas kernels, on_device(): pl.pallas_call(functools.partial(kernel, groups, layers, chunks, rows), o...  104 us

commit v1 on v0

v1 whole, which is shorter than its diff:
```python
import functools

import jax
import jax.numpy as jnp
from jax import lax
from jax.experimental import pallas as pl
from jax.experimental.pallas import tpu as pltpu
from jax.sharding import PartitionSpec as P

CORES = 2
LOCAL = 2
TILE_ROWS = 8


def plan(micro_count, capacity):
    per_chunk = max(1, 16 // capacity)
    later = -(-micro_count // per_chunk) - 1
    sizes = [micro_count - later * per_chunk] + [per_chunk] * later
    chunks, start, before = [], 0, 0
    for size in sizes:
        rows = -(-size * capacity // TILE_ROWS) * TILE_ROWS
        chunks.append((start, size, rows, before))
        start += size
        before += rows
    return chunks, before


def kernel(
    groups, layers, chunks, capacity,
    tok, gain_hbm, ids_hbm, slots_hbm, dropped_hbm, weigh_hbm, gate_hbm, up_hbm, down_hbm,
    out,
    gain, ids, slots, dropped, weigh, gate, up, down, rbuf, sbuf, pbuf, twin, rsum, retbuf, fbuf, whole, cin, hin, xin, hid, vals, cols,
    wsem, tok_sem, small_sem, disp_send, disp_recv, relay_send, twin_send, twin_recv, ret_send, ret_recv,
    next_send, next_recv, part_send, part_recv,
):
    count = len(chunks)
    chips = groups // CORES
    per_expert = chips // LOCAL
    micro_count, tok_rows, model_width = xin.shape
    width = gate.shape[-1]
    section = lax.axis_index("section")
    me = lax.axis_index("expert")
    layer = section // 2
    half = section % 2
    chip = me // CORES
    core = me % CORES
    mine_at = chip // per_expert
    sibling = me + 1 - 2 * core
    inner_layer = layer < layers - 1
    next_layer = lax.rem(layer + 1, layers)
    last_layer = lax.rem(layer - 1 + layers, layers)
    leads = (core == 1) & inner_layer

    def fetch(i):
        src, dst = ((gate_hbm, gate), (up_hbm, up), (down_hbm, down))[i]
        return pltpu.make_async_copy(src.at[0], dst, wsem.at[i])

    def small(i):
        src = (gain_hbm, ids_hbm, slots_hbm, dropped_hbm, weigh_hbm)[i]
        return pltpu.make_async_copy(src, (gain, ids, slots, dropped, weigh)[i], small_sem.at[i])

    def greet():
        barrier = pltpu.get_barrier_semaphore()

        def meet(**where):
            pl.semaphore_signal(barrier, inc=1, device_id=where, device_id_type=pl.DeviceIdType.MESH)

        def meet_layer(other):
            for to in range(2):
                meet(section=2 * other + to)

            @pl.when(core == 1)
            def _():
                for r in range(1, chips):
                    meet(section=2 * other + half, expert=chip_at(r) * CORES + core)

        for r in range(chips - 1, 0, -1):
            meet(expert=chip_at(r) * CORES + core)
        meet(section=2 * layer + 1 - half)

        @pl.when(inner_layer)
        def _():
            meet_layer(next_layer)

        @pl.when(layer > 0)
        def _():
            meet_layer(last_layer)

        meet(expert=sibling)
        beside = jnp.where(inner_layer, 1, 0) + jnp.where(layer > 0, 1, 0)
        pl.semaphore_wait(barrier, chips + 1 + beside * (2 + core * (chips - 1)))

    def load_tokens():
        return pltpu.make_async_copy(tok, xin, tok_sem)

    def span(base, index, size):
        return pl.ds(pl.multiple_of(base + index * size, TILE_ROWS), size)

    def remote(src, dst, send, recv, **where):
        return pltpu.make_async_remote_copy(
            src_ref=src, dst_ref=dst, send_sem=send, recv_sem=recv,
            device_id=where, device_id_type=pl.DeviceIdType.MESH,
        )

    def chip_at(r):
        return lax.rem(chip + r, chips)

    def held(c, place):
        rows, before = chunks[c][2:]
        return rbuf.at[span(before * groups, place, rows)]

    def outgoing(c, which, group):
        rows, before = chunks[c][2:]
        return sbuf.at[which, span(before * LOCAL, group, rows)]

    def direct(c, which, r, to):
        there = chip_at(r)
        place = core * chips + chip
        return remote(
            outgoing(c, which, there // per_expert), held(c, place), disp_send.at[which, c, r],
            disp_recv.at[c, place], section=2 * to + half, expert=there * CORES + core,
        )

    def own_rows(c):
        place = core * chips + chip
        return remote(
            outgoing(c, 0, mine_at), held(c, place), disp_send.at[0, c, 0], disp_recv.at[c, place], expert=sibling
        )

    def relay(c, r):
        place = core * chips + chip_at(r)
        return remote(held(c, place), held(c, place), relay_send.at[c, r], disp_recv.at[c, place], expert=sibling)

    def arrival(c, at_core, at_chip):
        place = at_core * chips + at_chip
        return remote(held(c, place), held(c, place), relay_send.at[c, 0], disp_recv.at[c, place], expert=sibling)

    def per_core(ref, c):
        rows, before = chunks[c][2:]
        return ref.at[pl.ds(before * chips, rows * chips)]

    def to_twin(c):
        rows, before = chunks[c][2:]
        return remote(
            pbuf.at[span(before * groups, 1 - core, rows * chips)], per_core(twin, c),
            twin_send.at[c], twin_recv.at[c], expert=sibling,
        )

    def back(ref, c, at_chip):
        rows, before = chunks[c][2:]
        return ref.at[span(before * chips, at_chip, rows)]

    def giving(c, r):
        there = chip_at(r)
        return remote(
            back(rsum, c, there), back(retbuf, c, chip), ret_send.at[c, r], ret_recv.at[c, chip],
            expert=there * CORES + core,
        )

    def given(c, r):
        there = chip_at(r)
        return remote(
            back(rsum, c, there), back(retbuf, c, there), ret_send.at[c, r], ret_recv.at[c, there],
            expert=there * CORES + core,
        )

    def micros(c):
        return pl.ds(chunks[c][0], chunks[c][1])

    def hand_on(c, to):
        return remote(
            fbuf.at[micros(c)], cin.at[half, micros(c)], next_send.at[to, c], next_recv.at[half, c],
            section=2 * next_layer + to,
        )

    def hand_whole(c):
        return remote(
            whole.at[micros(c)], cin.at[0, micros(c)], next_send.at[0, c], next_recv.at[0, c],
            section=2 * next_layer + half,
        )

    def handed(c, which):
        return remote(
            fbuf.at[micros(c)], cin.at[which, micros(c)], next_send.at[0, c], next_recv.at[which, c],
            section=2 * next_layer,
        )

    def to_partner(c):
        return remote(
            fbuf.at[micros(c)], hin.at[micros(c)], part_send.at[c], part_recv.at[c],
            section=2 * layer + 1 - half,
        )

    def position(c, turn, at_layer):
        start, _, rows, _ = chunks[c]
        at = start + turn
        local = ids[at_layer, at] - half * LOCAL
        owned = (dropped[at_layer, at] == 0) & (local >= 0) & (local < LOCAL)
        return jnp.where(owned, local * rows + turn * capacity + slots[at_layer, at], -1)

    def placed(c, states, at_layer):
        start, size, rows, _ = chunks[c]
        scale = gain[pl.ds(at_layer, 1), :]
        lines = lax.broadcasted_iota(jnp.int32, (LOCAL * rows, tok_rows), 0)
        sent = None
        for turn in range(size):
            current = states[start + turn].astype(jnp.float32)
            inv = lax.rsqrt(jnp.mean(current * current, axis=-1, keepdims=True) + 1e-05)
            normed = (current * inv * scale).astype(jnp.bfloat16)
            pos = position(c, turn, at_layer)
            hot = (lines == pos[0:1, :]) | (lines == pos[1:2, :])
            place = jnp.where(hot, 1.0, 0.0).astype(jnp.bfloat16)
            part = jnp.dot(place, normed, preferred_element_type=jnp.float32)
            sent = part if sent is None else sent + part
        return sent

    def dispatch(c):
        rows, before = chunks[c][2:]
        sent = placed(c, xin, layer)
        sbuf[0, pl.ds(before * LOCAL, LOCAL * rows), :] = sent.astype(jnp.bfloat16)
        own = jnp.where(mine_at == 0, sent[:rows], sent[rows:]).astype(jnp.bfloat16)
        rbuf[span(before * groups, core * chips + chip, rows), :] = own
        for r in range(chips - 1, 0, -1):
            direct(c, 0, r, layer).start()
        own_rows(c).start()

    def dispatch_over(c, which, states, to):
        rows, before = chunks[c][2:]
        sbuf[which, pl.ds(before * LOCAL, LOCAL * rows), :] = placed(c, states, to).astype(jnp.bfloat16)
        for r in range(chips - 1, -1, -1):
            direct(c, which, r, to).start()

    def columns():
        total = micro_count * tok_rows
        for c in range(count):
            for turn in range(chunks[c][1]):
                at = chunks[c][0] + turn
                vals[0, pl.ds(2 * at, 2), :] = position(c, turn, layer).astype(jnp.float32)
                vals[1, pl.ds(2 * at, 2), :] = weigh[layer, at]
        line = lax.broadcasted_iota(jnp.int32, (total, 2 * micro_count), 0)
        lane = lax.broadcasted_iota(jnp.int32, (total, 2 * micro_count), 1)
        small_line = lax.broadcasted_iota(jnp.int32, (total, tok_rows), 0)
        small_lane = lax.broadcasted_iota(jnp.int32, (total, tok_rows), 1)
        own = small_lane < 0
        for m in range(micro_count):
            own = own | (small_line == small_lane + m * tok_rows)
        for k in range(2):
            pick = lane < 0
            for m in range(micro_count):
                pick = pick | ((line >= m * tok_rows) & (line < (m + 1) * tok_rows) & (lane == 2 * m + k))
            pick = jnp.where(pick, 1.0, 0.0)
            for which in range(2):
                wide = jnp.dot(
                    pick, vals[which], precision=lax.Precision.HIGHEST, preferred_element_type=jnp.float32
                )
                cols[2 * k + which] = jnp.sum(jnp.where(own, wide, 0.0), axis=-1, keepdims=True)

    def forward(c):
        @pl.when(core == 1)
        def _():
            arrival(c, core, chip).wait_recv()
            relay(c, 0).start()

        for r in range(1, chips):
            arrival(c, core, chip_at(r)).wait_recv()
            relay(c, r).start()

    def compute(c):
        rows, before = chunks[c][2:]
        lines = rows * groups
        for r in range(chips):
            arrival(c, 1 - core, chip_at(r)).wait_recv()
        if c == 0:
            fetch(0).wait()
            fetch(1).wait()
        wide = 256 if width % 256 == 0 else 128

        def inner(t, carry):
            at = pl.ds(pl.multiple_of(t * wide, wide), wide)
            got = rbuf[pl.ds(before * groups, lines), :]
            g = jnp.dot(got, gate[:, at], preferred_element_type=jnp.float32)
            u = jnp.dot(got, up[:, at], preferred_element_type=jnp.float32)
            hid[pl.ds(0, lines), at] = (g / (1.0 + jnp.exp(-g)) * u).astype(jnp.bfloat16)
            return carry

        lax.fori_loop(0, width // wide, inner, 0, unroll=True)
        if c == 0:
            fetch(2).wait()

        def outer(t, carry):
            at = pl.ds(pl.multiple_of(t * 512, 512), 512)
            pbuf[pl.ds(before * groups, lines), at] = jnp.dot(
                hid[pl.ds(0, lines), :], down[:, at], preferred_element_type=jnp.float32
            ).astype(jnp.bfloat16)
            return carry

        lax.fori_loop(0, model_width // 512, outer, 0, unroll=True)
        to_twin(c).start()

    def pair(c):
        rows, before = chunks[c][2:]
        to_twin(c).wait_recv()
        mine = pbuf[span(before * groups, core, rows * chips), :].astype(jnp.float32)
        other = twin[pl.ds(before * chips, rows * chips), :].astype(jnp.float32)
        rsum[pl.ds(before * chips, rows * chips), :] = (mine + other).astype(jnp.bfloat16)
        for r in range(chips - 1, 0, -1):
            giving(c, r).start()
        retbuf[span(before * chips, chip, rows), :] = rsum[span(before * chips, chip, rows), :]

    def combine(c):
        start, size, rows, before = chunks[c]

        @pl.when((core == 1) & (layer > 0))
        def _():
            handed(c, 0).wait_recv()
            for turn in range(size):
                xin[start + turn] = cin[0, start + turn]

        for r in range(1, chips):
            given(c, r).wait_recv()
        parts = []
        for j in range(LOCAL):
            total = None
            for i in range(per_expert):
                low = before * chips + (j * per_expert + i) * rows
                piece = retbuf[pl.ds(low, rows), :].astype(jnp.float32)
                total = piece if total is None else total + piece
            parts.append(total)
        made = jnp.concatenate(parts, axis=0).astype(jnp.bfloat16)
        tokens = size * tok_rows
        lane = lax.broadcasted_iota(jnp.int32, (tokens, LOCAL * rows), 1).astype(jnp.float32)
        at = pl.ds(start * tok_rows, tokens)
        spread = jnp.zeros((tokens, LOCAL * rows), jnp.float32)
        for k in range(2):
            spread = spread + jnp.where(lane == cols[2 * k, at, :], cols[2 * k + 1, at, :], 0.0)
        coarse = spread.astype(jnp.bfloat16).astype(jnp.float32)
        both = jnp.concatenate([coarse, spread - coarse], axis=0).astype(jnp.bfloat16)
        share = jnp.dot(both, made, preferred_element_type=jnp.float32)
        share = share[:tokens] + share[tokens:]
        for turn in range(size):
            piece = share[turn * tok_rows : (turn + 1) * tok_rows]
            summed = xin[start + turn].astype(jnp.float32) + piece
            fbuf[start + turn] = jnp.where(half == 0, summed, piece).astype(jnp.bfloat16)

        @pl.when(inner_layer & (core == 0))
        def _():
            hand_on(c, 1).start()
            hand_on(c, 0).start()

        @pl.when(leads | ((half == 0) & (layer == layers - 1)))
        def _():
            to_partner(c).start()

        @pl.when(half == 0)
        def _():
            for turn in range(size):
                out[start + turn] = fbuf[start + turn]

    def total(c):
        start, size = chunks[c][:2]
        to_partner(c).wait_recv()
        for turn in range(size):
            at = start + turn
            whole[at] = (hin[at].astype(jnp.float32) + fbuf[at].astype(jnp.float32)).astype(jnp.bfloat16)

    def lead(c):
        @pl.when(leads)
        def _():
            total(c)
            dispatch_over(c, 1, whole, next_layer)
            hand_whole(c).start()

    def finish(c):
        start, size = chunks[c][:2]

        @pl.when((half == 1) & ~leads)
        def _():
            total(c)

        @pl.when(half == 1)
        def _():
            for turn in range(size):
                out[start + turn] = whole[start + turn]

    def first(c):
        if c < count:
            @pl.when((layer == 0) & (core == 0))
            def _():
                dispatch(c)

    def later(c):
        if c < count:
            start, size = chunks[c][:2]

            @pl.when((layer > 0) & (core == 0))
            def _():
                handed(c, 0).wait_recv()
                handed(c, 1).wait_recv()
                for turn in range(size):
                    at = start + turn
                    xin[at] = (cin[0, at].astype(jnp.float32) + cin[1, at].astype(jnp.float32)).astype(jnp.bfloat16)
                dispatch(c)

    helps = (layer == 1) & (core == 1)

    for i in range(5):
        small(i).start()

    @pl.when((layer == 0) | helps)
    def _():
        load_tokens().start()

    greet()
    for i in range(5):
        small(i).wait()

    @pl.when((layer == 0) | helps)
    def _():
        load_tokens().wait()

    for i in range(3):
        fetch(i).start()

    first(0)
    columns()

    @pl.when(helps)
    def _():
        for c in range(count):
            dispatch_over(c, 0, xin, 0)
            for r in range(chips):
                direct(c, 0, r, 0).wait_send()

    later(0)
    forward(0)
    first(1)
    first(2)
    for c in range(count):
        if c >= 1:
            later(c + 1)
        compute(c)
        if c == 0:
            later(1)
        if c >= 2:
            combine(c - 2)
        pair(c)
        first(c + 3)
        if c >= 2:
            lead(c - 2)
        if c + 1 < count:
            forward(c + 1)
    for c in range(max(count - 2, 0), count):
        combine(c)
        lead(c)
    @pl.when((half == 0) & (core == 0) & inner_layer)
    def _():
        for c in range(count):
            to_partner(c).start()

    for c in range(count):
        finish(c)

    for c in range(count):
        to_twin(c).wait_send()
        for r in range(1, chips):
            relay(c, r).wait_send()
            giving(c, r).wait_send()

    @pl.when(core == 0)
    def _():
        for c in range(count):
            own_rows(c).wait_send()
            for r in range(1, chips):
                direct(c, 0, r, layer).wait_send()

    @pl.when(core == 1)
    def _():
        for c in range(count):
            relay(c, 0).wait_send()

    @pl.when(leads)
    def _():
        for c in range(count):
            hand_whole(c).wait_send()
            for r in range(chips):
                direct(c, 1, r, next_layer).wait_send()

    @pl.when(inner_layer & (core == 0))
    def _():
        for c in range(count):
            hand_on(c, 0).wait_send()
            hand_on(c, 1).wait_send()

    @pl.when((half == 0) | leads)
    def _():
        for c in range(count):
            to_partner(c).wait_send()


def on_device(tokens, norm_gain, w_gate, w_up, w_down, expert_ids, slot_ids, dropped, gate_weights):
    groups = lax.axis_size("expert")
    layers = lax.axis_size("section") // 2
    micro_count, tok_rows, model_width = tokens.shape
    width = w_gate.shape[-1]
    capacity = 5 * tok_rows // (4 * LOCAL)
    chunks, total = plan(micro_count, capacity)
    chips = groups // CORES
    count = len(chunks)
    most = max(rows for _, _, rows, _ in chunks)

    def by_choice(value):
        return jnp.transpose(value, (0, 1, 3, 2))

    vm = pl.BlockSpec(memory_space=pltpu.VMEM)
    hb = pl.BlockSpec(memory_space=pl.ANY)
    half16 = jnp.bfloat16
    dma = pltpu.SemaphoreType.DMA
    choices = (layers, micro_count, 2, tok_rows)
    state = (micro_count, tok_rows, model_width)
    made = pl.pallas_call(
        functools.partial(kernel, groups, layers, chunks, capacity),
        out_shape=jax.ShapeDtypeStruct(state, half16),
        in_specs=[hb] * 9,
        out_specs=vm,
        scratch_shapes=[
            pltpu.VMEM(norm_gain.shape, jnp.float32),
            pltpu.VMEM(choices, jnp.int32),
            pltpu.VMEM(choices, jnp.int32),
            pltpu.VMEM(choices, jnp.int32),
            pltpu.VMEM(choices, jnp.float32),
            pltpu.VMEM((model_width, width), half16),
            pltpu.VMEM((model_width, width), half16),
            pltpu.VMEM((width, model_width), half16),
            pltpu.VMEM((total * groups, model_width), half16),
            pltpu.VMEM((2, total * LOCAL, model_width), half16),
            pltpu.VMEM((total * groups, model_width), half16),
            pltpu.VMEM((total * chips, model_width), half16),
            pltpu.VMEM((total * chips, model_width), half16),
            pltpu.VMEM((total * chips, model_width), half16),
            pltpu.VMEM(state, half16),
            pltpu.VMEM(state, half16),
            pltpu.VMEM((2,) + state, half16),
            pltpu.VMEM(state, half16),
            pltpu.VMEM(state, half16),
            pltpu.VMEM((groups * most, width), half16),
            pltpu.VMEM((2, 2 * micro_count, tok_rows), jnp.float32),
            pltpu.VMEM((4, micro_count * tok_rows, 1), jnp.float32),
            dma((3,)),
            dma,
            dma((5,)),
            dma((2, count, chips)),
            dma((count, groups)),
            dma((count, chips)),
            dma((count,)),
            dma((count,)),
            dma((count, chips)),
            dma((count, chips)),
            dma((2, count)),
            dma((2, count)),
            dma((count,)),
            dma((count,)),
        ],
        compiler_params=pltpu.CompilerParams(
            collective_id=0, has_side_effects=True, vmem_limit_bytes=58 * 1024 * 1024
        ),
    )(
        tokens, norm_gain, by_choice(expert_ids), by_choice(slot_ids), by_choice(dropped), by_choice(gate_weights),
        w_gate, w_up, w_down,
    )
    return made[None]


def solution(mesh):
    return jax.shard_map(
        on_device,
        mesh=mesh,
        in_specs=(
            P(None, "expert", None),
            P(),
            P("section", None, "expert"),
            P("section", None, "expert"),
            P("section", "expert", None),
            P(None, None, "expert", None),
            P(None, None, "expert", None),
            P(None, None, "expert", None),
            P(None, None, "expert", None),
        ),
        out_specs=P("section", None, "expert", None),
        check_vma=False,
    )
```

time: 115 us -> 76.2 us (0.66); the launches traced: 114 us -> 75.9 us
  Pallas kernels: 104 us -> 74.2 us
  local copies, waits for them, and re-layouts: 9.07 us -> 1.67 us
    pallas_call x1, Pallas kernels: 104 us -> 74.2 us  [on_device(): pl.pallas_call(functools.partial(kernel, groups, layers, chunks, capacity...]
    pad x6 -> x0, local copies, waits for them, and re-layouts: 3.02 us -> none  [the longest x3 2.04 us: chunked(): jnp.pad(value, [(0, 0), (0, lines - held)] + [(0, 0)] * len(rest), consta...]
    dynamic_slice x4 -> x0, local copies, waits for them, and re-layouts: 2.71 us -> none  [the longest x3 2.11 us: own_layer(): return lax.dynamic_index_in_dim(value, layer_at, 0, keepdims=False)]
where the time goes in v1:
time: 76.2 us; the launch traced here: 75.9 us
  Pallas kernels  74.2 us (97%)
  local copies, waits for them, and re-layouts  1.67 us (2%)
    pallas_call x1, Pallas kernels, on_device(): pl.pallas_call(functools.partial(kernel, groups, layers, chunks, capacity...  74.2 us
    unnamed x1, local copies, waits for them, and re-layouts  1.67 us

profile of v1, /device:TPU:6, one launch (start us, length us, event | category | flops | bytes accessed | tf_op | source)
XLA Modules:
  0.0 75.9 jit_solution(11353539247493181593)
XLA Ops:
  0.0 74.2 %shard_map.91 = bf16[8,8,2048]{2,1,0:T(8,128)(2,1)} custom-call(bf16[8,8,2048]{2,1,0:T(8,128)(2,1)} %tok.1, f32[2,2048]{1,0:T(2,128)} %gain_hbm.1, s32[2,8,2,8]{3,2,1,0:T(2,128)} %bitcast.6, s32[2,8,2,8]{3,2,1,0:T(2,128)} %bitcast.7, s32[2,8,2,8]{3,2,1,0:T(2,128)} %bitcast.8, f32[2,8,2,8]{3,2,1,0:T(2,128)} %bitcast.9, bf16[1,2048,1792]{2,1,0:T(8,128)(2,1)} %gate_hbm.1, ...), custom_call_target="tpu_custom_call" | custom-call | tf_op jit(solution)/shard_map/pallas_call | solution.py:520
  74.2 1.7 %copy.11 = bf16[1,8,8,2048]{3,2,1,0:T(8,128)(2,1)} copy(bf16[1,8,8,2048]{3,2,1,0:T(8,128)(2,1)} %bitcast.5) | data formatting | bytes 524288

commit v2 on v1

--- a/solution.py
+++ b/solution.py
@@ -10,6 +10,7 @@
 CORES = 2
 LOCAL = 2
 TILE_ROWS = 8
+DUE = ({2: (0,)}, {})
 
 
 def plan(micro_count, capacity):
@@ -49,7 +50,15 @@
     inner_layer = layer < layers - 1
     next_layer = lax.rem(layer + 1, layers)
     last_layer = lax.rem(layer - 1 + layers, layers)
-    leads = (core == 1) & inner_layer
+    helps = (layer == 1) & (core == 1)
+
+    def leads(c):
+        return inner_layer if c >= 1 else layer < 0
+
+    def places_own(c):
+        own = (layer == 0) & (core == 0)
+        return own | (layer > 0) if c == 0 else own
+
 
     def fetch(i):
         src, dst = ((gate_hbm, gate), (up_hbm, up), (down_hbm, down))[i]
@@ -69,10 +78,8 @@
             for to in range(2):
                 meet(section=2 * other + to)
 
-            @pl.when(core == 1)
-            def _():
-                for r in range(1, chips):
-                    meet(section=2 * other + half, expert=chip_at(r) * CORES + core)
+            for r in range(1, chips):
+                meet(section=2 * other + half, expert=chip_at(r) * CORES + core)
 
         for r in range(chips - 1, 0, -1):
             meet(expert=chip_at(r) * CORES + core)
@@ -88,7 +95,7 @@
 
         meet(expert=sibling)
         beside = jnp.where(inner_layer, 1, 0) + jnp.where(layer > 0, 1, 0)
-        pl.semaphore_wait(barrier, chips + 1 + beside * (2 + core * (chips - 1)))
+        pl.semaphore_wait(barrier, chips + 1 + beside * (chips + 1))
 
     def load_tokens():
         return pltpu.make_async_copy(tok, xin, tok_sem)
@@ -256,7 +263,7 @@
                 cols[2 * k + which] = jnp.sum(jnp.where(own, wide, 0.0), axis=-1, keepdims=True)
 
     def forward(c):
-        @pl.when(core == 1)
+        @pl.when(~places_own(c))
         def _():
             arrival(c, core, chip).wait_recv()
             relay(c, 0).start()
@@ -310,11 +317,12 @@
     def combine(c):
         start, size, rows, before = chunks[c]
 
-        @pl.when((core == 1) & (layer > 0))
-        def _():
-            handed(c, 0).wait_recv()
-            for turn in range(size):
-                xin[start + turn] = cin[0, start + turn]
+        if c >= 1:
+            @pl.when(layer > 0)
+            def _():
+                handed(c, 0).wait_recv()
+                for turn in range(size):
+                    xin[start + turn] = cin[0, start + turn]
 
         for r in range(1, chips):
             given(c, r).wait_recv()
@@ -342,12 +350,13 @@
             summed = xin[start + turn].astype(jnp.float32) + piece
             fbuf[start + turn] = jnp.where(half == 0, summed, piece).astype(jnp.bfloat16)
 
-        @pl.when(inner_layer & (core == 0))
-        def _():
-            hand_on(c, 1).start()
-            hand_on(c, 0).start()
-
-        @pl.when(leads | ((half == 0) & (layer == layers - 1)))
+        if c == 0:
+            @pl.when(inner_layer)
+            def _():
+                hand_on(c, 1).start()
+                hand_on(c, 0).start()
+
+        @pl.when(leads(c) | ((half == 0) & (layer == layers - 1)))
         def _():
             to_partner(c).start()
 
@@ -364,7 +373,7 @@
             whole[at] = (hin[at].astype(jnp.float32) + fbuf[at].astype(jnp.float32)).astype(jnp.bfloat16)
 
     def lead(c):
-        @pl.when(leads)
+        @pl.when(leads(c))
         def _():
             total(c)
             dispatch_over(c, 1, whole, next_layer)
@@ -373,7 +382,7 @@
     def finish(c):
         start, size = chunks[c][:2]
 
-        @pl.when((half == 1) & ~leads)
+        @pl.when((half == 1) & ~leads(c))
         def _():
             total(c)
 
@@ -392,7 +401,7 @@
         if c < count:
             start, size = chunks[c][:2]
 
-            @pl.when((layer > 0) & (core == 0))
+            @pl.when(layer > 0)
             def _():
                 handed(c, 0).wait_recv()
                 handed(c, 1).wait_recv()
@@ -401,8 +410,6 @@
                     xin[at] = (cin[0, at].astype(jnp.float32) + cin[1, at].astype(jnp.float32)).astype(jnp.bfloat16)
                 dispatch(c)
 
-    helps = (layer == 1) & (core == 1)
-
     for i in range(5):
         small(i).start()
 
@@ -435,27 +442,29 @@
     forward(0)
     first(1)
     first(2)
+    early, late = DUE
+    done = []
     for c in range(count):
-        if c >= 1:
-            later(c + 1)
         compute(c)
-        if c == 0:
-            later(1)
-        if c >= 2:
-            combine(c - 2)
+        for other in early.get(c, ()):
+            combine(other)
         pair(c)
         first(c + 3)
-        if c >= 2:
-            lead(c - 2)
+        for other in late.get(c, ()):
+            combine(other)
+        for other in early.get(c, ()) + late.get(c, ()):
+            lead(other)
+            done.append(other)
         if c + 1 < count:
             forward(c + 1)
-    for c in range(max(count - 2, 0), count):
-        combine(c)
-        lead(c)
-    @pl.when((half == 0) & (core == 0) & inner_layer)
+    for c in range(count):
+        if c not in done:
+            combine(c)
+            lead(c)
+
+    @pl.when((half == 0) & inner_layer)
     def _():
-        for c in range(count):
-            to_partner(c).start()
+        to_partner(0).start()
 
     for c in range(count):
         finish(c)
@@ -466,35 +475,31 @@
             relay(c, r).wait_send()
             giving(c, r).wait_send()
 
-    @pl.when(core == 0)
-    def _():
-        for c in range(count):
+    for c in range(count):
+        @pl.when(places_own(c))
+        def _():
             own_rows(c).wait_send()
             for r in range(1, chips):
                 direct(c, 0, r, layer).wait_send()
 
-    @pl.when(core == 1)
-    def _():
-        for c in range(count):
+        @pl.when(~places_own(c))
+        def _():
             relay(c, 0).wait_send()
 
-    @pl.when(leads)
-    def _():
-        for c in range(count):
+        @pl.when(leads(c))
+        def _():
             hand_whole(c).wait_send()
             for r in range(chips):
                 direct(c, 1, r, next_layer).wait_send()
 
-    @pl.when(inner_layer & (core == 0))
+        @pl.when((half == 0) | leads(c))
+        def _():
+            to_partner(c).wait_send()
+
+    @pl.when(inner_layer)
     def _():
-        for c in range(count):
-            hand_on(c, 0).wait_send()
-            hand_on(c, 1).wait_send()
-
-    @pl.when((half == 0) | leads)
-    def _():
-        for c in range(count):
-            to_partner(c).wait_send()
+        hand_on(0, 0).wait_send()
+        hand_on(0, 1).wait_send()
 
 
 def on_device(tokens, norm_gain, w_gate, w_up, w_down, expert_ids, slot_ids, dropped, gate_weights):

time: 76.2 us -> 69.5 us (0.912)
  Pallas kernels: 74.2 us -> 67.5 us
    pallas_call x1, Pallas kernels: 74.2 us -> 67.5 us  [on_device(): pl.pallas_call(functools.partial(kernel, groups, layers, chunks, capacity...]
where the time goes in v2:
time: 69.5 us; the launch traced here: 69.2 us
  Pallas kernels  67.5 us (97%)
  local copies, waits for them, and re-layouts  1.67 us (2%)
    pallas_call x1, Pallas kernels, on_device(): pl.pallas_call(functools.partial(kernel, groups, layers, chunks, capacity...  67.5 us
    unnamed x1, local copies, waits for them, and re-layouts  1.67 us

profile of v2, /device:TPU:6, one launch (start us, length us, event | category | flops | bytes accessed | tf_op | source)
XLA Modules:
  0.0 69.2 jit_solution(6774848773263393405)
XLA Ops:
  0.0 67.5 %shard_map.91 = bf16[8,8,2048]{2,1,0:T(8,128)(2,1)} custom-call(bf16[8,8,2048]{2,1,0:T(8,128)(2,1)} %tok.1, f32[2,2048]{1,0:T(2,128)} %gain_hbm.1, s32[2,8,2,8]{3,2,1,0:T(2,128)} %bitcast.6, s32[2,8,2,8]{3,2,1,0:T(2,128)} %bitcast.7, s32[2,8,2,8]{3,2,1,0:T(2,128)} %bitcast.8, f32[2,8,2,8]{3,2,1,0:T(2,128)} %bitcast.9, bf16[1,2048,1792]{2,1,0:T(8,128)(2,1)} %gate_hbm.1, ...), custom_call_target="tpu_custom_call" | custom-call | tf_op jit(solution)/shard_map/pallas_call | solution.py:525
  67.5 1.7 %copy.11 = bf16[1,8,8,2048]{3,2,1,0:T(8,128)(2,1)} copy(bf16[1,8,8,2048]{3,2,1,0:T(8,128)(2,1)} %bitcast.5) | data formatting | bytes 524288

commit v3 on v2

--- a/solution.py
+++ b/solution.py
@@ -50,15 +50,14 @@
     inner_layer = layer < layers - 1
     next_layer = lax.rem(layer + 1, layers)
     last_layer = lax.rem(layer - 1 + layers, layers)
-    helps = (layer == 1) & (core == 1)
-
     def leads(c):
         return inner_layer if c >= 1 else layer < 0
 
+    def helps(c):
+        return layer == 1 if c >= 1 else (layer == 1) & (core == 1)
+
     def places_own(c):
-        own = (layer == 0) & (core == 0)
-        return own | (layer > 0) if c == 0 else own
-
+        return layer < 0 if c >= 1 else (layer > 0) | (core == 0)
 
     def fetch(i):
         src, dst = ((gate_hbm, gate), (up_hbm, up), (down_hbm, down))[i]
@@ -392,28 +391,26 @@
                 out[start + turn] = whole[start + turn]
 
     def first(c):
-        if c < count:
-            @pl.when((layer == 0) & (core == 0))
-            def _():
-                dispatch(c)
+        @pl.when((layer == 0) & (core == 0))
+        def _():
+            dispatch(c)
 
     def later(c):
-        if c < count:
-            start, size = chunks[c][:2]
-
-            @pl.when(layer > 0)
-            def _():
-                handed(c, 0).wait_recv()
-                handed(c, 1).wait_recv()
-                for turn in range(size):
-                    at = start + turn
-                    xin[at] = (cin[0, at].astype(jnp.float32) + cin[1, at].astype(jnp.float32)).astype(jnp.bfloat16)
-                dispatch(c)
+        start, size = chunks[c][:2]
+
+        @pl.when(layer > 0)
+        def _():
+            handed(c, 0).wait_recv()
+            handed(c, 1).wait_recv()
+            for turn in range(size):
+                at = start + turn
+                xin[at] = (cin[0, at].astype(jnp.float32) + cin[1, at].astype(jnp.float32)).astype(jnp.bfloat16)
+            dispatch(c)
 
     for i in range(5):
         small(i).start()
 
-    @pl.when((layer == 0) | helps)
+    @pl.when(layer < 2)
     def _():
         load_tokens().start()
 
@@ -421,7 +418,7 @@
     for i in range(5):
         small(i).wait()
 
-    @pl.when((layer == 0) | helps)
+    @pl.when(layer < 2)
     def _():
         load_tokens().wait()
 
@@ -431,17 +428,15 @@
     first(0)
     columns()
 
-    @pl.when(helps)
-    def _():
-        for c in range(count):
+    for c in range(count):
+        @pl.when(helps(c))
+        def _():
             dispatch_over(c, 0, xin, 0)
             for r in range(chips):
                 direct(c, 0, r, 0).wait_send()
 
     later(0)
     forward(0)
-    first(1)
-    first(2)
     early, late = DUE
     done = []
     for c in range(count):
@@ -449,7 +444,6 @@
         for other in early.get(c, ()):
             combine(other)
         pair(c)
-        first(c + 3)
         for other in late.get(c, ()):
             combine(other)
         for other in early.get(c, ()) + late.get(c, ()):

time: 69.5 us -> 69.1 us (level)
  no operation moved by 1% of the time
where the time goes in v3:
time: 69.1 us; the launch traced here: 69 us
  Pallas kernels  67.3 us (97%)
  local copies, waits for them, and re-layouts  1.67 us (2%)
    pallas_call x1, Pallas kernels, on_device(): pl.pallas_call(functools.partial(kernel, groups, layers, chunks, capacity...  67.3 us
    unnamed x1, local copies, waits for them, and re-layouts  1.67 us

profile of v3, /device:TPU:6, one launch (start us, length us, event | category | flops | bytes accessed | tf_op | source)
XLA Modules:
  0.0 69.0 jit_solution(543773677703462236)
XLA Ops:
  0.0 67.3 %shard_map.91 = bf16[8,8,2048]{2,1,0:T(8,128)(2,1)} custom-call(bf16[8,8,2048]{2,1,0:T(8,128)(2,1)} %tok.1, f32[2,2048]{1,0:T(2,128)} %gain_hbm.1, s32[2,8,2,8]{3,2,1,0:T(2,128)} %bitcast.6, s32[2,8,2,8]{3,2,1,0:T(2,128)} %bitcast.7, s32[2,8,2,8]{3,2,1,0:T(2,128)} %bitcast.8, f32[2,8,2,8]{3,2,1,0:T(2,128)} %bitcast.9, bf16[1,2048,1792]{2,1,0:T(8,128)(2,1)} %gate_hbm.1, ...), custom_call_target="tpu_custom_call" | custom-call | tf_op jit(solution)/shard_map/pallas_call | solution.py:519
  67.3 1.7 %copy.11 = bf16[1,8,8,2048]{3,2,1,0:T(8,128)(2,1)} copy(bf16[1,8,8,2048]{3,2,1,0:T(8,128)(2,1)} %bitcast.5) | data formatting | bytes 524288
